TPU v7x, 32 devices: a whole 2x2x4 slice. The times are simulated.
32 devices in a mesh: groups: 2 (over y), seq: 8 (over z, x), tp: 2 (over core).
Axes of the slice: x: 2, y: 2, z: 4, core: 2. Of those that a mesh axis runs over, the one named last changes fastest.
Arguments:
- span_queries: bfloat16 [128, 64, 128], P(('groups', 'seq'), 'tp'), parts along dimension 0, may hold values from -180 to 180
- span_keys: bfloat16 [128, 4, 128], P(('groups', 'seq'), 'tp'), parts along dimension 0, may hold values from -9 to 9
- span_values: bfloat16 [128, 4, 128], P(('groups', 'seq'), 'tp'), parts along dimension 0, may hold values from -6.5 to 6.5
- prefix_keys: bfloat16 [1152, 4, 128], P(('groups', 'seq'), 'tp'), parts along dimension 0, may hold values from -9 to 9
- prefix_values: bfloat16 [1152, 4, 128], P(('groups', 'seq'), 'tp'), parts along dimension 0, may hold values from -6.5 to 6.5
- prefix_lengths: int32 [16], P('groups'), parts along dimension 0, may hold values from 1 to 72
- decode_queries: bfloat16 [32, 64, 128], P(('groups', 'seq'), 'tp'), parts along dimension 0, may hold values from -180 to 180
- decode_new_keys: bfloat16 [32, 4, 128], P(('groups', 'seq'), 'tp'), parts along dimension 0, may hold values from -6 to 6
- decode_new_values: bfloat16 [32, 4, 128], P(('groups', 'seq'), 'tp'), parts along dimension 0, may hold values from -6 to 6
- decode_key_cache: bfloat16 [64, 256, 4, 128], P(('groups', 'seq'), None, 'tp'), parts along dimension 0, may hold values from -6 to 6
- decode_value_cache: bfloat16 [64, 256, 4, 128], P(('groups', 'seq'), None, 'tp'), parts along dimension 0, may hold values from -6 to 6
- owner_map: int32 [32, 1], P('groups'), parts along dimension 0, may hold values from 0 to 7; in each aligned block of 16 rows (0 to 15, 16 to 31, ...) at most 4 rows name the same one
- decode_lengths: int32 [32], P('groups'), parts along dimension 0, may hold values from 1 to 256
Outputs:
- prefill_out: bfloat16 [128, 64, 128], P(('groups', 'seq'), 'tp'), parts along dimension 0
- decode_out: bfloat16 [64, 64, 128], P(('groups', 'seq'), 'tp'), parts along dimension 0
There are 2 independent parts, one for each index of `groups`. A program takes and returns all parts, laid end to end along the dimension named above; each array names one. Nothing has to cross between parts.
Inputs may be any that keep to these rules, and one draw needn't show every extreme that they name: `owner_map`: no shard owns more than 4 requests, and some shard owns exactly 4.
All inputs are finite; a program needn't handle non-finite values.
Results may differ from a plain program's by a relative error of at most 0.005.
Values may be sent and summed in bfloat16 or wider, within the bound.
No kernel may reach another device: no remote copies, remote signals or barrier semaphores. Data moves between devices by JAX's collectives and lax.ppermute only.
A program may use at most 64 MiB of HBM per device.

v0:
```python
import jax
import jax.numpy as jnp
from jax import lax
from jax.sharding import PartitionSpec as P

LOWEST = -1e30


def lookup_small(table, wanted):
    columns = jnp.arange(table.shape[0], dtype=jnp.int32)
    return jnp.sum(jnp.where(wanted[:, None] == columns[None, :], table[None, :], 0), axis=1)


def block_split(length):
    blocks = 1
    while length // blocks > 512 or length % blocks != 0:
        blocks += 1
    return blocks


def online_step(carried, queries, key_rows, value_rows, allowed):
    running_max, normalizer, weighted = carried
    scale = queries.shape[-1] ** (-0.5)
    scores = (
        jnp.einsum("tkgd,nkd->tkgn", queries, key_rows, preferred_element_type=jnp.float32) * scale
    )
    visible = allowed[:, None, None, :]
    scores = jnp.where(visible, scores, LOWEST)
    new_max = jnp.maximum(running_max, jnp.max(scores, axis=-1))
    weights = jnp.where(visible, jnp.exp(scores - new_max[..., None]), 0.0)
    factor = jnp.exp(running_max - new_max)
    normalizer = normalizer * factor + jnp.sum(weights, axis=-1)
    weighted = weighted * factor[..., None] + jnp.einsum(
        "tkgn,nkd->tkgd",
        weights.astype(jnp.bfloat16),
        value_rows,
        preferred_element_type=jnp.float32,
    )
    return (new_max, normalizer, weighted)


def guarded_step(carried, queries, key_rows, value_rows, allowed):
    return lax.cond(
        jnp.any(allowed),
        lambda inner: online_step(inner, queries, key_rows, value_rows, allowed),
        lambda inner: inner,
        carried,
    )


def fold_rows(carried, queries, key_rows, value_rows, allowed):
    length = key_rows.shape[0]
    blocks = block_split(length)
    if blocks == 1:
        return guarded_step(carried, queries, key_rows, value_rows, allowed)
    width = length // blocks
    stacked = (
        key_rows.reshape((blocks, width) + key_rows.shape[1:]),
        value_rows.reshape((blocks, width) + value_rows.shape[1:]),
        allowed.reshape(allowed.shape[0], blocks, width).transpose(1, 0, 2),
    )

    def visit(inner_carry, parts):
        return (guarded_step(inner_carry, queries, parts[0], parts[1], parts[2]), None)

    carried, unused = lax.scan(visit, carried, stacked)
    return carried


def on_device(
    span_queries,
    span_keys,
    span_values,
    prefix_keys,
    prefix_values,
    prefix_lengths,
    decode_queries,
    decode_new_keys,
    decode_new_values,
    decode_key_cache,
    decode_value_cache,
    owner_map,
    decode_lengths,
):
    device = lax.axis_index("seq")
    tokens_here, heads_here, head_dim = span_queries.shape
    kv_here = span_keys.shape[1]
    group_size = heads_here // kv_here
    queries = span_queries.reshape(tokens_here, kv_here, group_size, head_dim)
    token_index = device * tokens_here + jnp.arange(tokens_here, dtype=jnp.int32)
    prefix_here = prefix_keys.shape[0]
    initial = (
        jnp.full((tokens_here, kv_here, group_size), LOWEST, jnp.float32),
        jnp.zeros((tokens_here, kv_here, group_size), jnp.float32),
        jnp.zeros((tokens_here, kv_here, group_size, head_dim), jnp.float32),
    )
    stride = prefix_here + tokens_here
    both_keys = jnp.concatenate([prefix_keys, span_keys], axis=0)
    both_values = jnp.concatenate([prefix_values, span_values], axis=0)
    carried = initial
    key_rows = lax.all_gather(both_keys, "seq", axis=0, tiled=True)
    value_rows = lax.all_gather(both_values, "seq", axis=0, tiled=True)
    length = key_rows.shape[0]
    shards = length // stride
    tail = key_rows.shape[1:]
    keys_split = key_rows.reshape((shards, stride) + tail)
    values_split = value_rows.reshape((shards, stride) + tail)
    prefix_k = keys_split[:, :prefix_here].reshape((shards * prefix_here,) + tail)
    prefix_v = values_split[:, :prefix_here].reshape((shards * prefix_here,) + tail)
    span_k = keys_split[:, prefix_here:].reshape((shards * tokens_here,) + tail)
    span_v = values_split[:, prefix_here:].reshape((shards * tokens_here,) + tail)
    prefix_position = jnp.arange(shards * prefix_here, dtype=jnp.int32)
    prefix_ok = prefix_position % prefix_here < lookup_small(
        prefix_lengths, prefix_position // prefix_here
    )
    carried = fold_rows(
        carried,
        queries,
        prefix_k,
        prefix_v,
        jnp.broadcast_to(prefix_ok[None, :], (tokens_here, prefix_k.shape[0])),
    )
    span_position = jnp.arange(shards * tokens_here, dtype=jnp.int32)
    carried = fold_rows(
        carried, queries, span_k, span_v, span_position[None, :] <= token_index[:, None]
    )
    running_max, normalizer, weighted = carried
    prefill_out = (
        (weighted / normalizer[..., None])
        .reshape(tokens_here, heads_here, head_dim)
        .astype(jnp.bfloat16)
    )
    owners = owner_map[:, 0]
    requests = owners.shape[0]
    order = jnp.arange(requests, dtype=jnp.int32)
    earlier = (owners[None, :] == owners[:, None]) & (order[None, :] < order[:, None])
    ranking = jnp.sum(earlier.astype(jnp.int32), axis=1)
    slots_here = decode_key_cache.shape[0]
    slot_ids = jnp.arange(slots_here, dtype=jnp.int32)
    query_rows = lax.all_gather(decode_queries, "seq", axis=0, tiled=True)
    new_keys = lax.all_gather(decode_new_keys, "seq", axis=0, tiled=True)
    new_values = lax.all_gather(decode_new_values, "seq", axis=0, tiled=True)
    chosen = (owners == device)[None, :] & (ranking[None, :] == slot_ids[:, None])
    selector = chosen.astype(jnp.bfloat16)
    picked_queries = jnp.einsum(
        "sn,nhd->shd", selector, query_rows, preferred_element_type=jnp.float32
    )
    picked_keys = jnp.einsum("sn,nkd->skd", selector, new_keys, preferred_element_type=jnp.float32)
    picked_values = jnp.einsum(
        "sn,nkd->skd", selector, new_values, preferred_element_type=jnp.float32
    )
    picked_lengths = jnp.sum(jnp.where(chosen, decode_lengths[None, :], 0), axis=1)
    context = decode_key_cache.shape[1]
    grouped = picked_queries.astype(jnp.bfloat16).reshape(slots_here, kv_here, group_size, head_dim)
    own_keys = picked_keys.astype(jnp.bfloat16)
    own_values = picked_values.astype(jnp.bfloat16)
    scale = head_dim ** (-0.5)
    scores = (
        jnp.einsum("skgd,sckd->skgc", grouped, decode_key_cache, preferred_element_type=jnp.float32)
        * scale
    )
    visible = (jnp.arange(context, dtype=jnp.int32)[None, :] < picked_lengths[:, None])[
        :, None, None, :
    ]
    scores = jnp.where(visible, scores, LOWEST)
    own_score = (
        jnp.einsum("skgd,skd->skg", grouped, own_keys, preferred_element_type=jnp.float32) * scale
    )
    top_score = jnp.maximum(jnp.max(scores, axis=-1), own_score)
    weights = jnp.where(visible, jnp.exp(scores - top_score[..., None]), 0.0)
    own_weight = jnp.exp(own_score - top_score)
    total_weight = jnp.sum(weights, axis=-1) + own_weight
    rounded_own = lax.optimization_barrier(own_weight.astype(jnp.bfloat16)).astype(jnp.float32)
    mixed = jnp.einsum(
        "skgc,sckd->skgd",
        weights.astype(jnp.bfloat16),
        decode_value_cache,
        preferred_element_type=jnp.float32,
    )
    mixed = mixed + rounded_own[..., None] * own_values.astype(jnp.float32)[:, :, None, :]
    count_here = jnp.sum((owners == device).astype(jnp.int32))
    used = (slot_ids < count_here)[:, None, None, None]
    decode_out = (
        jnp.where(used, mixed / total_weight[..., None], 0.0)
        .reshape(slots_here, heads_here, head_dim)
        .astype(jnp.bfloat16)
    )
    return (prefill_out, decode_out)


def solution(mesh):
    return jax.shard_map(
        on_device,
        mesh=mesh,
        in_specs=(
            P(("groups", "seq"), "tp", None),
            P(("groups", "seq"), "tp", None),
            P(("groups", "seq"), "tp", None),
            P(("groups", "seq"), "tp", None),
            P(("groups", "seq"), "tp", None),
            P("groups"),
            P(("groups", "seq"), "tp", None),
            P(("groups", "seq"), "tp", None),
            P(("groups", "seq"), "tp", None),
            P(("groups", "seq"), None, "tp", None),
            P(("groups", "seq"), None, "tp", None),
            P("groups", None),
            P("groups"),
        ),
        out_specs=(P(("groups", "seq"), "tp", None), P(("groups", "seq"), "tp", None)),
        check_vma=False,
    )
```

profile of v0, /device:TPU:0, one launch (start us, length us, event | category | flops | bytes accessed | tf_op | source)
XLA Modules:
  0.0 148.8 jit_solution(11207647977653412298)
XLA Ops:
  0.7 0.7 iota_compare_fusion.3
  2.0 0.7 select_reduce_fusion
  2.9 0.7 copy-done.5
  3.6 32.7 %all_gather.15 = bf16[640,2,128]{2,1,0:T(2,128)(2,1)S(1)} all-gather(bf16[80,2,128]{2,1,0:T(2,128)(2,1)S(1)} %pad_maximum_fusion), channel_id=1, replica_groups=mesh['groups'=2,'seq'=8,'tp'=2] {'seq'}, dimensions={0}, use_global_device_ids=true | all-gather | bytes 368640 | tf_op jit(solution)/shard_map/all_gather | solution.py:101
  36.4 0.8 copy-done.1
  37.2 0.8 copy-done.3
  38.1 30.9 %all_gather.16 = bf16[640,2,128]{2,1,0:T(2,128)(2,1)S(1)} all-gather(bf16[80,2,128]{2,1,0:T(2,128)(2,1)S(1)} %pad_maximum_fusion.1), channel_id=1, replica_groups=mesh['groups'=2,'seq'=8,'tp'=2] {'seq'}, dimensions={0}, use_global_device_ids=true | all-gather | bytes 368640 | tf_op jit(solution)/shard_map/all_gather | solution.py:102
  69.1 4.4 %while.14 = (s32[]{:T(128)}, f32[8,2,16]{2,0,1:T(8,128)S(1)}, f32[8,2,16]{2,0,1:T(8,128)S(1)}, f32[8,2,16,128]{3,2,0,1:T(8,128)S(1)}, pred[2,8,288]{2,1,0:T(8,12...) while((s32[]{:T(128)}, f32[8,2,16]{2,0,1:T(8,128)S(1)}, ...), condition=%wide.region_8.9_spmd, body=%wide.region_2.8_spmd.sunk | while | flops 38480640 | bytes 1649647 | solution.py:66
  69.2 0.7 fusion.72
  70.5 0.9 conditional.4
  71.4 0.7 fusion.72
  72.7 0.9 conditional.4
  73.6 0.7 conditional.2
  74.5 0.6 copy.71
  75.2 30.5 %all_gather.17 = bf16[16,32,128]{2,1,0:T(8,128)(2,1)S(1)} all-gather(bf16[2,32,128]{2,1,0:T(8,128)(2,1)S(1)} %copy-done.4), channel_id=1, replica_groups=mesh['groups'=2,'seq'=8,'tp'=2] {'seq'}, dimensions={0}, use_global_device_ids=true | all-gather | bytes 147456 | tf_op jit(solution)/shard_map/all_gather | solution.py:140
  105.7 0.7 copy-done.10
  106.5 0.6 convert_reduce_fusion.1
  107.2 0.7 copy-done.9
  108.5 0.7 copy-done.7
  109.2 20.5 %all_gather.18 = bf16[16,2,128]{2,1,0:T(2,128)(2,1)S(1)} all-gather(bf16[2,2,128]{2,1,0:T(2,128)(2,1)S(1)} %copy-done.7), channel_id=1, replica_groups=mesh['groups'=2,'seq'=8,'tp'=2] {'seq'}, dimensions={0}, use_global_device_ids=true | all-gather | bytes 9216 | tf_op jit(solution)/shard_map/all_gather | solution.py:141
  130.2 0.7 copy-done.8
  130.8 16.3 %all_gather.19 = bf16[16,2,128]{2,1,0:T(2,128)(2,1)S(1)} all-gather(bf16[2,2,128]{2,1,0:T(2,128)(2,1)S(1)} %copy-done.8), channel_id=1, replica_groups=mesh['groups'=2,'seq'=8,'tp'=2] {'seq'}, dimensions={0}, use_global_device_ids=true | all-gather | bytes 9216 | tf_op jit(solution)/shard_map/all_gather | solution.py:142
  147.2 0.6 iota_compare_fusion.5
  147.9 0.9 fusion.34
  (65 shorter events, 4.5 us)
Async XLA Ops:
  0.6 107.6 %copy-start = (bf16[4,256,2,128]{3,2,1,0:T(2,128)(2,1)S(1)}, bf16[4,256,2,128]{3,2,1,0:T(2,128)(2,1)}, u32[]{:S(2)}) copy-start(bf16[4,256,2,128]{3,2,1,0:T(2,128)(2,1)} %param.28) | copy-start | bytes 1572868
  0.6 2.3 %copy-start.2 = (bf16[72,2,128]{2,1,0:T(2,128)(2,1)S(1)}, bf16[72,2,128]{2,1,0:T(2,128)(2,1)}, u32[]{:S(2)}) copy-start(bf16[72,2,128]{2,1,0:T(2,128)(2,1)} %param.22) | copy-start | bytes 110596
  2.9 0.7 copy-start.5
  36.4 0.8 copy-start.1
  37.2 0.8 copy-start.3
  37.2 0.8 copy-start.6
  74.5 0.7 copy-start.4
  105.7 0.7 copy-start.10
  107.2 0.7 copy-start.9
  108.1 39.8 %copy-start.11 = (bf16[4,256,2,128]{3,2,1,0:T(2,128)(2,1)S(1)}, bf16[4,256,2,128]{3,2,1,0:T(2,128)(2,1)}, u32[]{:S(2)}) copy-start(bf16[4,256,2,128]{3,2,1,0:T(2,128)(2,1)} %param.29) | copy-start | bytes 1572868
  108.5 0.7 copy-start.7
  130.1 0.7 copy-start.8
where the time goes:
time: 149 us
  blocking collectives  131 us (88%)
  local copies, waits for them, and re-layouts  5.93 us (4%)
  other arithmetic  5.57 us (4%)
  matrix products  3.39 us (2%)
  between operations  1.53 us (1%)
  loops' own time  1.5 us (1%)
    all_gather x1, blocking collectives, on_device(): key_rows = lax.all_gather(both_keys, 'seq', axis=0, tiled=True)  32.7 us
    all_gather x1, blocking collectives, on_device(): value_rows = lax.all_gather(both_values, 'seq', axis=0, tiled=True)  30.9 us
    all_gather x1, blocking collectives, on_device(): query_rows = lax.all_gather(decode_queries, 'seq', axis=0, tiled=True)  30.5 us
    all_gather x1, blocking collectives, on_device(): new_keys = lax.all_gather(decode_new_keys, 'seq', axis=0, tiled=True)  20.5 us
    all_gather x1, blocking collectives, on_device(): new_values = lax.all_gather(decode_new_values, 'seq', axis=0, tiled=True)  16.3 us
    unnamed x24, local copies, waits for them, and re-layouts  4.99 us

commit v1 on v0

--- a/solution.py
+++ b/solution.py
@@ -137,14 +137,25 @@
     ranking = jnp.sum(earlier.astype(jnp.int32), axis=1)
     slots_here = decode_key_cache.shape[0]
     slot_ids = jnp.arange(slots_here, dtype=jnp.int32)
-    query_rows = lax.all_gather(decode_queries, "seq", axis=0, tiled=True)
     new_keys = lax.all_gather(decode_new_keys, "seq", axis=0, tiled=True)
     new_values = lax.all_gather(decode_new_values, "seq", axis=0, tiled=True)
     chosen = (owners == device)[None, :] & (ranking[None, :] == slot_ids[:, None])
     selector = chosen.astype(jnp.bfloat16)
-    picked_queries = jnp.einsum(
-        "sn,nhd->shd", selector, query_rows, preferred_element_type=jnp.float32
-    )
+    count, index, width_2 = (lax.axis_size("seq"), lax.axis_index("seq"), decode_queries.shape[0])
+    right = [(i, (i + 1) % count) for i in range(count)]
+    carried_2, picked_queries = (decode_queries, None)
+    for step in range(count):
+        upcoming = lax.ppermute(carried_2, "seq", right) if step < count - 1 else None
+        absorb = jnp.einsum(
+            "sn,nhd->shd",
+            lax.dynamic_slice_in_dim(
+                selector, (index - step) % count * width_2, carried_2.shape[0], axis=1
+            ),
+            carried_2,
+            preferred_element_type=jnp.float32,
+        )
+        picked_queries = absorb if picked_queries is None else picked_queries + absorb
+        carried_2 = upcoming
     picked_keys = jnp.einsum("sn,nkd->skd", selector, new_keys, preferred_element_type=jnp.float32)
     picked_values = jnp.einsum(
         "sn,nkd->skd", selector, new_values, preferred_element_type=jnp.float32

time: 149 us -> 158 us (1.060)
  waiting for transfers between devices: 0 us -> 35.3 us
  blocking collectives: 131 us -> 97.3 us
  starting transfers between devices: 0 us -> 5.05 us
  matrix products: 3.39 us -> 5.25 us
    ppermute x0 -> x7, waiting for transfers between devices: none -> 35.3 us  [on_device(): lax.ppermute(carried_2, 'seq', right)]
    all_gather x1 -> x0, blocking collectives: 30.5 us -> none  [on_device(): query_rows = lax.all_gather(decode_queries, 'seq', axis=0, tiled=True)]
    ppermute x0 -> x7, starting transfers between devices: none -> 5.05 us  [on_device(): lax.ppermute(carried_2, 'seq', right)]
    unnamed x24 -> x27, local copies, waits for them, and re-layouts: 4.99 us -> 5.23 us
  transfers between devices with their start and end apart: 0 -> 7, of which waited for: 0 -> 6; matrix products, arithmetic and copies ran while one was open for 0% -> 6% of each run, Pallas kernels for 0% -> 0%
where the time goes in v1:
time: 158 us; the launch traced here: 157 us
  blocking collectives  97.3 us (62%)
  waiting for transfers between devices  35.3 us (22%)
  local copies, waits for them, and re-layouts  6.16 us (4%)
  matrix products  5.25 us (3%)
  starting transfers between devices  5.05 us (3%)
  other arithmetic  4.9 us (3%)
  between operations  1.71 us (1%)
    ppermute x7, waiting for transfers between devices, on_device(): lax.ppermute(carried_2, 'seq', right)  35.3 us
    all_gather x1, blocking collectives, on_device(): key_rows = lax.all_gather(both_keys, 'seq', axis=0, tiled=True)  31.2 us
    all_gather x1, blocking collectives, on_device(): value_rows = lax.all_gather(both_values, 'seq', axis=0, tiled=True)  30.9 us
    all_gather x1, blocking collectives, on_device(): new_keys = lax.all_gather(decode_new_keys, 'seq', axis=0, tiled=True)  19 us
    all_gather x1, blocking collectives, on_device(): new_values = lax.all_gather(decode_new_values, 'seq', axis=0, tiled=True)  16.3 us
    unnamed x27, local copies, waits for them, and re-layouts  5.23 us
    ppermute x7, starting transfers between devices, on_device(): lax.ppermute(carried_2, 'seq', right)  5.05 us
  transfers between devices with their start and end apart: 7, of which 6 were waited for; matrix products, arithmetic and copies ran while one was open for 6% of the time, Pallas kernels for 0%

profile of v1, /device:TPU:0, one launch (start us, length us, event | category | flops | bytes accessed | tf_op | source)
XLA Modules:
  0.0 157.0 jit_solution(15006418897313105475)
XLA Ops:
  0.6 0.8 copy.82
  1.4 3.0 %collective-permute-start = (bf16[2,32,128]{2,0,1:T(2,128)(2,1)S(1)}, bf16[2,32,128]{2,0,1:T(2,128)(2,1)S(1)}, u32[]{:S(2)}, u32[]{:S(2)}) collective-permute-start(bf16[2,32,128]{2,0,1:T(2,128)(2,1)S(1)} %copy.82), channel_id=1, source_target_pairs={{0,2},{2,4},{4,6},{6,8},{8,10},{10,12},{12,14},{14,0},{1,3},{3,5},... | collective-permute-start | bytes 49160 | tf_op jit(solution)/shard_map/ppermute | solution.py:148
  4.5 0.7 iota_compare_fusion.4
  6.1 0.7 copy-done.5
  6.8 31.2 %all_gather.12 = bf16[640,2,128]{2,1,0:T(2,128)(2,1)S(1)} all-gather(bf16[80,2,128]{2,1,0:T(2,128)(2,1)S(1)} %pad_maximum_fusion), channel_id=1, replica_groups=mesh['groups'=2,'seq'=8,'tp'=2] {'seq'}, dimensions={0}, use_global_device_ids=true | all-gather | bytes 368640 | tf_op jit(solution)/shard_map/all_gather | solution.py:101
  38.1 0.8 copy-done.1
  38.9 0.8 copy-done.4
  39.7 30.9 %all_gather.13 = bf16[640,2,128]{2,1,0:T(2,128)(2,1)S(1)} all-gather(bf16[80,2,128]{2,1,0:T(2,128)(2,1)S(1)} %pad_maximum_fusion.1), channel_id=1, replica_groups=mesh['groups'=2,'seq'=8,'tp'=2] {'seq'}, dimensions={0}, use_global_device_ids=true | all-gather | bytes 368640 | tf_op jit(solution)/shard_map/all_gather | solution.py:102
  70.8 4.2 %while.14 = (s32[]{:T(128)}, f32[8,2,16]{2,0,1:T(8,128)S(1)}, f32[8,2,16]{2,0,1:T(8,128)S(1)}, f32[8,2,16,128]{3,2,0,1:T(8,128)S(1)}, pred[2,8,288]{2,1,0:T(8,12...) while((s32[]{:T(128)}, f32[8,2,16]{2,0,1:T(8,128)S(1)}, ...), condition=%wide.region_8.9_spmd, body=%wide.region_2.8_spmd.sunk | while | flops 38480640 | bytes 1649647 | solution.py:66
  72.0 0.9 conditional.4
  74.1 0.9 conditional.4
  77.2 19.0 %all_gather.14 = bf16[16,2,128]{2,1,0:T(2,128)(2,1)S(1)} all-gather(bf16[2,2,128]{2,1,0:T(2,128)(2,1)S(1)} %copy-done.7), channel_id=1, replica_groups=mesh['groups'=2,'seq'=8,'tp'=2] {'seq'}, dimensions={0}, use_global_device_ids=true | all-gather | bytes 9216 | tf_op jit(solution)/shard_map/all_gather | solution.py:140
  96.9 16.3 %all_gather.15 = bf16[16,2,128]{2,1,0:T(2,128)(2,1)S(1)} all-gather(bf16[2,2,128]{2,1,0:T(2,128)(2,1)S(1)} %copy-done.8), channel_id=1, replica_groups=mesh['groups'=2,'seq'=8,'tp'=2] {'seq'}, dimensions={0}, use_global_device_ids=true | all-gather | bytes 9216 | tf_op jit(solution)/shard_map/all_gather | solution.py:141
  113.5 0.7 conditional.2
  115.1 0.7 iota_compare_fusion.5
  115.9 0.6 copy.81
  116.6 2.0 %collective-permute-start.1 = (bf16[2,32,128]{2,0,1:T(2,128)(2,1)S(1)}, bf16[2,32,128]{2,0,1:T(2,128)(2,1)S(1)}, u32[]{:S(2)}, u32[]{:S(2)}) collective-permute-start(bf16[2,32,128]{2,0,1:T(2,128)(2,1)S(1)} %collective-permute-done), channel_id=1, source_target_pairs={{0,2},{2,4},{4,6},{6,8},{8,10},{10,12},{12,14},{14,0},{1,3},{3,5},... | collective-permute-start | bytes 49160 | tf_op jit(solution)/shard_map/ppermute | solution.py:148
  118.8 4.2 %collective-permute-done.1 = bf16[2,32,128]{2,0,1:T(2,128)(2,1)S(1)} collective-permute-done((bf16[2,32,128]{2,0,1:T(2,128)(2,1)S(1)}, bf16[2,32,128]{2,0,1:T(2,128)(2,1)S(1)}, u32[]{:S(2)}, u32[]{:S(2)}) %collective-permute-start.1) | collective-permute-done | bytes 16416 | tf_op jit(solution)/shard_map/ppermute | solution.py:148
  123.2 6.2 %collective-permute-done.2 = bf16[2,32,128]{2,0,1:T(2,128)(2,1)S(1)} collective-permute-done((bf16[2,32,128]{2,0,1:T(2,128)(2,1)S(1)}, bf16[2,32,128]{2,0,1:T(2,128)(2,1)S(1)}, u32[]{:S(2)}, u32[]{:S(2)}) %collective-permute-start.2) | collective-permute-done | bytes 16416 | tf_op jit(solution)/shard_map/ppermute | solution.py:148
  129.7 6.2 %collective-permute-done.3 = bf16[2,32,128]{2,0,1:T(2,128)(2,1)S(1)} collective-permute-done((bf16[2,32,128]{2,0,1:T(2,128)(2,1)S(1)}, bf16[2,32,128]{2,0,1:T(2,128)(2,1)S(1)}, u32[]{:S(2)}, u32[]{:S(2)}) %collective-permute-start.3) | collective-permute-done | bytes 16416 | tf_op jit(solution)/shard_map/ppermute | solution.py:148
  136.1 6.2 %collective-permute-done.4 = bf16[2,32,128]{2,0,1:T(2,128)(2,1)S(1)} collective-permute-done((bf16[2,32,128]{2,0,1:T(2,128)(2,1)S(1)}, bf16[2,32,128]{2,0,1:T(2,128)(2,1)S(1)}, u32[]{:S(2)}, u32[]{:S(2)}) %collective-permute-start.4) | collective-permute-done | bytes 16416 | tf_op jit(solution)/shard_map/ppermute | solution.py:148
  142.6 6.2 %collective-permute-done.5 = bf16[2,32,128]{2,0,1:T(2,128)(2,1)S(1)} collective-permute-done((bf16[2,32,128]{2,0,1:T(2,128)(2,1)S(1)}, bf16[2,32,128]{2,0,1:T(2,128)(2,1)S(1)}, u32[]{:S(2)}, u32[]{:S(2)}) %collective-permute-start.5) | collective-permute-done | bytes 16416 | tf_op jit(solution)/shard_map/ppermute | solution.py:148
  149.0 6.2 %collective-permute-done.6 = bf16[2,32,128]{2,0,1:T(2,128)(2,1)S(1)} collective-permute-done((bf16[2,32,128]{2,0,1:T(2,128)(2,1)S(1)}, bf16[2,32,128]{2,0,1:T(2,128)(2,1)S(1)}, u32[]{:S(2)}, u32[]{:S(2)}) %collective-permute-start.6) | collective-permute-done | bytes 16416 | tf_op jit(solution)/shard_map/ppermute | solution.py:148
  156.1 0.9 fusion.34
  (89 shorter events, 10.5 us)
Async XLA Ops:
  0.6 154.9 %copy-start = (bf16[4,256,2,128]{3,2,1,0:T(2,128)(2,1)S(1)}, bf16[4,256,2,128]{3,2,1,0:T(2,128)(2,1)}, u32[]{:S(2)}) copy-start(bf16[4,256,2,128]{3,2,1,0:T(2,128)(2,1)} %param.28) | copy-start | bytes 1572868
  1.4 4.6 %copy-start.3 = (bf16[72,2,128]{2,1,0:T(2,128)(2,1)S(1)}, bf16[72,2,128]{2,1,0:T(2,128)(2,1)}, u32[]{:S(2)}) copy-start(bf16[72,2,128]{2,1,0:T(2,128)(2,1)} %param.22) | copy-start | bytes 110596
  1.4 115.1 %collective-permute-start = (bf16[2,32,128]{2,0,1:T(2,128)(2,1)S(1)}, bf16[2,32,128]{2,0,1:T(2,128)(2,1)S(1)}, u32[]{:S(2)}, u32[]{:S(2)}) collective-permute-start(bf16[2,32,128]{2,0,1:T(2,128)(2,1)S(1)} %copy.82), channel_id=1, source_target_pairs={{0,2},{2,4},{4,6},{6,8},{8,10},{10,12},{12,14},{14,0},{1,3},{3,5},... | collective-permute-start | bytes 49160 | tf_op jit(solution)/shard_map/ppermute | solution.py:148
  5.2 0.7 copy-start.9
  6.0 0.7 copy-start.5
  38.0 0.8 copy-start.1
  38.9 0.8 copy-start.4
  38.9 0.8 copy-start.6
  70.7 4.2 %copy-start.10 = (s32[16,1]{0,1:T(1,128)S(1)}, s32[16,1]{0,1:T(1,128)}, u32[]{:S(2)}) copy-start(s32[16,1]{0,1:T(1,128)} %param.30) | copy-start | bytes 196
  75.8 0.7 copy-start.11
  76.6 0.7 copy-start.7
  96.3 0.7 copy-start.8
  114.2 0.7 copy-start.2
  116.6 6.4 %collective-permute-start.1 = (bf16[2,32,128]{2,0,1:T(2,128)(2,1)S(1)}, bf16[2,32,128]{2,0,1:T(2,128)(2,1)S(1)}, u32[]{:S(2)}, u32[]{:S(2)}) collective-permute-start(bf16[2,32,128]{2,0,1:T(2,128)(2,1)S(1)} %collective-permute-done), channel_id=1, source_target_pairs={{0,2},{2,4},{4,6},{6,8},{8,10},{10,12},{12,14},{14,0},{1,3},{3,5},... | collective-permute-start | bytes 49160 | tf_op jit(solution)/shard_map/ppermute | solution.py:148
  123.0 6.4 %collective-permute-start.2 = (bf16[2,32,128]{2,0,1:T(2,128)(2,1)S(1)}, bf16[2,32,128]{2,0,1:T(2,128)(2,1)S(1)}, u32[]{:S(2)}, u32[]{:S(2)}) collective-permute-start(bf16[2,32,128]{2,0,1:T(2,128)(2,1)S(1)} %collective-permute-done.1), channel_id=1, source_target_pairs={{0,2},{2,4},{4,6},{6,8},{8,10},{10,12},{12,14},{14,0},{1,3},{3,5},... | collective-permute-start | bytes 49160 | tf_op jit(solution)/shard_map/ppermute | solution.py:148
  129.5 6.4 %collective-permute-start.3 = (bf16[2,32,128]{2,0,1:T(2,128)(2,1)S(1)}, bf16[2,32,128]{2,0,1:T(2,128)(2,1)S(1)}, u32[]{:S(2)}, u32[]{:S(2)}) collective-permute-start(bf16[2,32,128]{2,0,1:T(2,128)(2,1)S(1)} %collective-permute-done.2), channel_id=1, source_target_pairs={{0,2},{2,4},{4,6},{6,8},{8,10},{10,12},{12,14},{14,0},{1,3},{3,5},... | collective-permute-start | bytes 49160 | tf_op jit(solution)/shard_map/ppermute | solution.py:148
  135.9 6.4 %collective-permute-start.4 = (bf16[2,32,128]{2,0,1:T(2,128)(2,1)S(1)}, bf16[2,32,128]{2,0,1:T(2,128)(2,1)S(1)}, u32[]{:S(2)}, u32[]{:S(2)}) collective-permute-start(bf16[2,32,128]{2,0,1:T(2,128)(2,1)S(1)} %collective-permute-done.3), channel_id=1, source_target_pairs={{0,2},{2,4},{4,6},{6,8},{8,10},{10,12},{12,14},{14,0},{1,3},{3,5},... | collective-permute-start | bytes 49160 | tf_op jit(solution)/shard_map/ppermute | solution.py:148
  142.3 6.4 %collective-permute-start.5 = (bf16[2,32,128]{2,0,1:T(2,128)(2,1)S(1)}, bf16[2,32,128]{2,0,1:T(2,128)(2,1)S(1)}, u32[]{:S(2)}, u32[]{:S(2)}) collective-permute-start(bf16[2,32,128]{2,0,1:T(2,128)(2,1)S(1)} %collective-permute-done.4), channel_id=1, source_target_pairs={{0,2},{2,4},{4,6},{6,8},{8,10},{10,12},{12,14},{14,0},{1,3},{3,5},... | collective-permute-start | bytes 49160 | tf_op jit(solution)/shard_map/ppermute | solution.py:148
  148.8 6.4 %collective-permute-start.6 = (bf16[2,32,128]{2,0,1:T(2,128)(2,1)S(1)}, bf16[2,32,128]{2,0,1:T(2,128)(2,1)S(1)}, u32[]{:S(2)}, u32[]{:S(2)}) collective-permute-start(bf16[2,32,128]{2,0,1:T(2,128)(2,1)S(1)} %collective-permute-done.5), channel_id=1, source_target_pairs={{0,2},{2,4},{4,6},{6,8},{8,10},{10,12},{12,14},{14,0},{1,3},{3,5},... | collective-permute-start | bytes 49160 | tf_op jit(solution)/shard_map/ppermute | solution.py:148
  149.0 7.2 %copy-start.12 = (bf16[4,256,2,128]{3,2,1,0:T(2,128)(2,1)S(1)}, bf16[4,256,2,128]{3,2,1,0:T(2,128)(2,1)}, u32[]{:S(2)}) copy-start(bf16[4,256,2,128]{3,2,1,0:T(2,128)(2,1)} %param.29) | copy-start | bytes 1572868
